TPU v7x, 256 devices: a whole 4x4x8 slice. The times are simulated.
256 devices in a mesh: row: 8 (over x, core), col: 32 (over y, z).
Axes of the slice: x: 4, y: 4, z: 8, core: 2. Of those that a mesh axis runs over, the one named last changes fastest.
Arguments:
- rhs: float32 [8, 32, 8, 4, 128], P('row', 'col'), may hold values from -6 to 6
- diag0: float32 [8, 32, 8, 128], P('row', 'col'), may hold values from 2 to 4
- blocks0: float32 [8, 32, 8, 14, 128, 128], P('row', 'col'), may hold values from -0.1875 to 0.1875
- cols0: int32 [8, 32, 8, 14], P('row', 'col'), may hold values from 0 to 23
- sends0: int32 [8, 32, 4, 4], P('row', 'col'), may hold values from 0 to 7
- pro0: float32 [8, 32, 8, 128, 128], P('row', 'col'), may hold values from -0.5 to 0.5
- agg0: int32 [8, 32, 8], P('row', 'col'), may hold values from 0 to 1
- diag1: float32 [8, 32, 2, 128], P('row', 'col'), may hold values from 2 to 4
- blocks1: float32 [8, 32, 2, 14, 128, 128], P('row', 'col'), may hold values from -0.1875 to 0.1875
- cols1: int32 [8, 32, 2, 14], P('row', 'col'), may hold values from 0 to 9
- sends1: int32 [8, 32, 4, 2], P('row', 'col'), may hold values from 0 to 1
- pro1: float32 [8, 32, 2, 128, 128], P('row', 'col'), may hold values from -0.25 to 0.25
- agg1: int32 [8, 32, 2], P('row', 'col'), may hold values from 0 to 63
- cinv: float32 [8192, 8192], P(('row', 'col')), may hold values from -0.0625 to 0.0625
Outputs:
- solution: float32 [8, 32, 8, 4, 128], P('row', 'col')
Inputs may be any that keep to these rules, and one draw needn't show every extreme that they name: `sends0`: indices of the sender's own fine blocks. `sends1`: indices of the sender's own level-one blocks. `cols0`: indices into the extended fine vector of 24 blocks. `cols1`: indices into the extended level-one vector of 10 blocks. `agg0`: a level-one block of the same partition. `agg1`: a coarsest block, on any partition.
All inputs are finite; a program needn't handle non-finite values.
Results may differ from a plain program's by a relative error of at most 0.0001.
Values sent between devices are 32-bit elements; how exact they have to be, the bound alone decides.
A program may use at most 64 MiB of HBM per device.

v0:
```python
import functools
import jax
import jax.numpy as jnp
from jax import lax
from jax.sharding import Mesh
from jax.sharding import PartitionSpec as P

NU = 2
ROW_COL = ("row_0", "row_1", "col_0", "col_1")
ROW = ("row_0", "row_1")
COL = ("col_0", "col_1")
HIGH = lax.Precision.HIGHEST
OMEGA = 0.3


def extended_2(value, sides, width):
    edges = {}
    for axis, dim in sides:
        size, length = (lax.axis_size(axis), value.shape[dim])
        up = [(i, (i + 1) % size) for i in range(size - 1)]
        last = lax.slice_in_dim(value, length - width, length, axis=dim)
        leading = lax.slice_in_dim(value, 0, width, axis=dim)
        edges[dim] = (
            lax.ppermute(last, axis, up),
            lax.ppermute(leading, axis, [(b, a) for a, b in up]),
        )
    done = []
    for _, dim in sides:
        low, high = edges[dim]
        around = [(width, width) if d in done else (0, 0) for d in range(value.ndim)]
        value = jnp.concatenate([jnp.pad(low, around), value, jnp.pad(high, around)], axis=dim)
        done.append(dim)
    return value


def by_axis(value, axes):
    return functools.reduce(lax.psum, axes, value)


def gather_ghosts(vector, sends):
    packed = vector[sends]
    padded = extended_2(packed[None, None], ((ROW, 0), (COL, 1)), 1)
    return jnp.concatenate(
        [vector, padded[0, 1, 0], padded[2, 1, 1], padded[1, 0, 2], padded[1, 2, 3]], axis=0
    )


def apply_op(vector, diag, blocks, cols, sends):
    extended = gather_ghosts(vector, sends)
    nearby = extended[cols]
    coupled = jnp.einsum("bkij,bkrj->bri", blocks, nearby, precision=HIGH)
    return diag[:, None, :] * vector + coupled


def smooth(vector, right_side, diag, blocks, cols, sends, count):
    for sweep in range(count):
        vector = (
            vector
            + OMEGA * (right_side - apply_op(vector, diag, blocks, cols, sends)) / diag[:, None, :]
        )
    return vector


def on_device(
    rhs, diag0, blocks0, cols0, sends0, pro0, agg0, diag1, blocks1, cols1, sends1, pro1, agg1, cinv
):
    fine_rhs = rhs[0, 0]
    fine_diag = diag0[0, 0]
    fine_blocks = blocks0[0, 0]
    fine_cols = cols0[0, 0]
    fine_sends = sends0[0, 0]
    fine_pro = pro0[0, 0]
    level_diag = diag1[0, 0]
    level_blocks = blocks1[0, 0]
    level_cols = cols1[0, 0]
    level_sends = sends1[0, 0]
    level_pro = pro1[0, 0]
    level_count = level_diag.shape[0]
    block_size = level_diag.shape[1]
    loads = fine_rhs.shape[1]
    coarse_total = cinv.shape[1]
    coarse_count = coarse_total // block_size
    fine_x = OMEGA * fine_rhs / fine_diag[:, None, :]
    fine_x = smooth(fine_x, fine_rhs, fine_diag, fine_blocks, fine_cols, fine_sends, NU - 1)
    fine_res = fine_rhs - apply_op(fine_x, fine_diag, fine_blocks, fine_cols, fine_sends)
    onehot0 = (agg0[0, 0][:, None] == jnp.arange(level_count)).astype(jnp.float32)
    restricted = jnp.einsum("bij,bri->brj", fine_pro, fine_res, precision=HIGH)
    level_rhs = jnp.einsum("bc,brj->crj", onehot0, restricted, precision=HIGH)
    level_x = OMEGA * level_rhs / level_diag[:, None, :]
    level_x = smooth(level_x, level_rhs, level_diag, level_blocks, level_cols, level_sends, NU - 1)
    level_res = level_rhs - apply_op(level_x, level_diag, level_blocks, level_cols, level_sends)
    onehot1 = (agg1[0, 0][:, None] == jnp.arange(coarse_count)).astype(jnp.float32)
    contrib = jnp.einsum("bij,bri->brj", level_pro, level_res, precision=HIGH)
    term = jnp.einsum("bc,brj->rcj", onehot1, contrib, precision=HIGH).reshape(loads, coarse_total)
    coarse_rhs = by_axis(term, ROW_COL)
    own_rows = jnp.einsum("ij,rj->ri", cinv, coarse_rhs, precision=HIGH)
    coarse_x = lax.all_gather(own_rows, ROW_COL, axis=1, tiled=True)
    coarse_blocks = coarse_x.reshape(loads, coarse_count, block_size)
    picked = jnp.einsum("bc,rcj->brj", onehot1, coarse_blocks, precision=HIGH)
    level_x = level_x + jnp.einsum("bij,brj->bri", level_pro, picked, precision=HIGH)
    level_x = smooth(level_x, level_rhs, level_diag, level_blocks, level_cols, level_sends, NU)
    lifted = jnp.einsum("bc,crj->brj", onehot0, level_x, precision=HIGH)
    fine_x = fine_x + jnp.einsum("bij,brj->bri", fine_pro, lifted, precision=HIGH)
    fine_x = smooth(fine_x, fine_rhs, fine_diag, fine_blocks, fine_cols, fine_sends, NU)
    return fine_x[None, None]


def solution(mesh):
    finer = Mesh(mesh.devices.reshape(4, 2, 4, 8), ("row_0", "row_1", "col_0", "col_1"))
    in_specs = (
        P(ROW, COL, None, None, None),
        P(ROW, COL, None, None),
        P(ROW, COL, None, None, None, None),
        P(ROW, COL, None, None),
        P(ROW, COL, None, None),
        P(ROW, COL, None, None, None),
        P(ROW, COL, None),
        P(ROW, COL, None, None),
        P(ROW, COL, None, None, None, None),
        P(ROW, COL, None, None),
        P(ROW, COL, None, None),
        P(ROW, COL, None, None, None),
        P(ROW, COL, None),
        P(ROW_COL, None),
    )
    out_specs = P(ROW, COL, None, None, None)
    return jax.shard_map(
        on_device, mesh=finer, in_specs=in_specs, out_specs=out_specs, check_vma=False
    )
```

profile of v0, /device:TPU:8, one launch (start us, length us, event | category | flops | bytes accessed | tf_op | source)
XLA Modules:
  0.0 488.9 jit_solution(9224719478229903555)
XLA Ops:
  10.3 7.6 %collective-permute-start.3 = (f32[1,1,4,4,4,128]{5,4,3,2,1,0:T(4,128)S(1)}, f32[1,1,4,4,4,128]{5,4,3,2,1,0:T(4,128)S(1)}, u32[]{:S(2)}, u32[]{:S(2)}) collective-permute-start(f32[1,1,4,4,4,128]{5,4,3,2,1,0:T(4,128)S(1)} %bitcast.456), channel_id=1, source_target_pairs={{1,0},{2,1},{3,2},{4,3},{5,4},{6,5},{7,6},{8,7},{9,8},{10,9},{11,1... | collective-permute-start | bytes 98312 | tf_op jit(solution)/shard_map/ppermute | solution.py:25
  17.9 1.9 collective-permute-start.2
  21.1 3.0 collective-permute-start
  26.6 8.3 %constant_dynamic-update-slice_fusion.9 = (f32[24,4,128]{2,1,0:T(4,128)S(1)}, f32[8,4,128]{2,1,0:T(4,128)S(1)}) fusion(f32[8,14,4,128]{3,2,1,0:T(4,128)S(1)} %bitcast.438, f32[1,1,8,14,128,128]{5,4,3,2,1,0:T(8,128)} %param.16, f32[8,128]{1,0:T(8,128)} %bitcast.448, f32[1,1,8,4,128]{4,3,2,1,0:T(4,128)} %param.14), kind=kOutput, calls=%fused_computation.98 | convolution fusion | flops 88113152 | bytes 7622656 | tf_op jit(solution)/shard_map/bkij,bkrj->bri/dot_general | solution.py:51
  35.5 3.0 collective-permute-start.4
  39.2 6.0 %collective-permute-start.7 = (f32[1,1,4,4,4,128]{5,4,3,2,1,0:T(4,128)S(1)}, f32[1,1,4,4,4,128]{5,4,3,2,1,0:T(4,128)S(1)}, u32[]{:S(2)}, u32[]{:S(2)}) collective-permute-start(f32[1,1,4,4,4,128]{5,4,3,2,1,0:T(4,128)S(1)} %bitcast.461), channel_id=1, source_target_pairs={{1,0},{2,1},{3,2},{4,3},{5,4},{6,5},{7,6},{8,7},{9,8},{10,9},{11,1... | collective-permute-start | bytes 98312 | tf_op jit(solution)/shard_map/ppermute | solution.py:25
  45.2 1.9 collective-permute-start.6
  49.2 2.0 collective-permute-done.5
  51.2 1.9 collective-permute-done.6
  54.6 9.2 %fusion.64 = f32[8,4,128]{2,1,0:T(4,128)S(1)} fusion(f32[8,14,4,128]{3,2,1,0:T(4,128)} %bitcast.440, f32[1,1,8,14,128,128]{5,4,3,2,1,0:T(8,128)} %param.16, f32[1,1,8,4,128]{4,3,2,1,0:T(4,128)S(1)} %copy-done.4, f32[8,4,128]{2,1,0:T(4,128)} %copy-done.5, f32[8,128]{1,0:T(8,128)} %bitcast.449), kind=kOutput, calls=%fused_computation.50 | convolution fusion | flops 88092672 | bytes 7622656 | tf_op jit(solution)/shard_map/bkij,bkrj->bri/dot_general | solution.py:51
  67.0 2.0 gather_fusion.4
  69.7 2.6 collective-permute-start.8
  73.6 5.7 %collective-permute-start.11 = (f32[1,1,4,2,4,128]{5,4,3,2,1,0:T(4,128)S(1)}, f32[1,1,4,2,4,128]{5,4,3,2,1,0:T(4,128)S(1)}, u32[]{:S(2)}, u32[]{:S(2)}) collective-permute-start(f32[1,1,4,2,4,128]{5,4,3,2,1,0:T(4,128)S(1)} %copy.98), channel_id=1, source_target_pairs={{1,0},{2,1},{3,2},{4,3},{5,4},{6,5},{7,6},{8,7},{9,8},{10,9},{11,1... | collective-permute-start | bytes 49160 | tf_op jit(solution)/shard_map/ppermute | solution.py:25
  79.3 1.9 collective-permute-start.10
  84.9 2.1 collective-permute-done.10
  88.2 2.1 gather_fusion.5
  90.3 3.1 constant_dynamic-update-slice_fusion.19
  93.4 2.0 gather_fusion.6
  96.1 1.9 collective-permute-start.12
  98.0 5.7 %collective-permute-start.15 = (f32[1,1,4,2,4,128]{5,4,3,2,1,0:T(4,128)S(1)}, f32[1,1,4,2,4,128]{5,4,3,2,1,0:T(4,128)S(1)}, u32[]{:S(2)}, u32[]{:S(2)}) collective-permute-start(f32[1,1,4,2,4,128]{5,4,3,2,1,0:T(4,128)S(1)} %copy.104), channel_id=1, source_target_pairs={{1,0},{2,1},{3,2},{4,3},{5,4},{6,5},{7,6},{8,7},{9,8},{10,9},{11,1... | collective-permute-start | bytes 49160 | tf_op jit(solution)/shard_map/ppermute | solution.py:25
  103.7 1.9 collective-permute-start.14
  109.3 2.1 collective-permute-done.14
  112.7 2.1 gather_fusion.7
  114.7 2.4 fusion.127
  119.2 44.8 %all-reduce.5.cloned.1.call-done = f32[4,8192]{1,0:T(4,128)} async-done(((f32[4,8192]{1,0:T(4,128)}), f32[4,8192]{1,0:T(4,128)}) %all-reduce.5.cloned.1.call-update) | async-done | bytes 131088 | tf_op jit(solution)/shard_map/psum | solution.py:37
  164.1 31.7 %all-reduce.7.cloned.1.call-done = f32[4,8192]{1,0:T(4,128)} async-done(((f32[4,8192]{1,0:T(4,128)}), f32[4,8192]{1,0:T(4,128)}) %all-reduce.7.cloned.1.call-update) | async-done | bytes 131088 | tf_op jit(solution)/shard_map/psum | solution.py:37
  195.9 49.0 %all-reduce.9.cloned.1.call-done = f32[4,8192]{1,0:T(4,128)} async-done(((f32[4,8192]{1,0:T(4,128)}), f32[4,8192]{1,0:T(4,128)}) %all-reduce.9.cloned.1.call-update) | async-done | bytes 131088 | tf_op jit(solution)/shard_map/psum | solution.py:37
  244.8 76.3 %all-reduce.11.cloned.1.call-done = f32[4,8192]{1,0:T(4,128)} async-done(((f32[4,8192]{1,0:T(4,128)}), f32[4,8192]{1,0:T(4,128)}) %all-reduce.11.cloned.1.call-update) | async-done | bytes 131088 | tf_op jit(solution)/shard_map/psum | solution.py:37
  321.2 1.8 convolution_bitcast_fusion.1
  323.0 70.0 %all-gather = f32[256,32,4]{1,2,0:T(4,128)S(1)} all-gather(f32[1,32,4]{1,2,0:T(4,128)S(1)} %convolution_bitcast_fusion.1), channel_id=1, replica_groups=mesh['row_0'=4,'row_1'=2,'col_0'=4,'col_1'=8] {'row_0','row_1','col_0','..., dimensions={0}, use_global_device_ids=true | all-gather | bytes 131584 | tf_op jit(solution)/shard_map/all_gather | solution.py:97
  397.2 4.6 collective-permute-start.19
  401.8 1.9 collective-permute-start.18
  405.0 1.8 collective-permute-done.17
  406.8 2.7 collective-permute-done.18
  410.2 2.3 constant_dynamic-update-slice_fusion.29
  414.6 4.9 %collective-permute-start.23 = (f32[1,1,4,2,4,128]{5,4,3,2,1,0:T(4,128)S(1)}, f32[1,1,4,2,4,128]{5,4,3,2,1,0:T(4,128)S(1)}, u32[]{:S(2)}, u32[]{:S(2)}) collective-permute-start(f32[1,1,4,2,4,128]{5,4,3,2,1,0:T(4,128)S(1)} %copy.119), channel_id=1, source_target_pairs={{1,0},{2,1},{3,2},{4,3},{5,4},{6,5},{7,6},{8,7},{9,8},{10,9},{11,1... | collective-permute-start | bytes 49160 | tf_op jit(solution)/shard_map/ppermute | solution.py:25
  419.5 1.9 collective-permute-start.22
  424.5 2.7 collective-permute-done.22
  428.0 2.3 fusion.106
  434.7 5.7 %collective-permute-start.27 = (f32[1,1,4,4,4,128]{5,4,3,2,1,0:T(4,128)S(1)}, f32[1,1,4,4,4,128]{5,4,3,2,1,0:T(4,128)S(1)}, u32[]{:S(2)}, u32[]{:S(2)}) collective-permute-start(f32[1,1,4,4,4,128]{5,4,3,2,1,0:T(4,128)S(1)} %bitcast.469), channel_id=1, source_target_pairs={{1,0},{2,1},{3,2},{4,3},{5,4},{6,5},{7,6},{8,7},{9,8},{10,9},{11,1... | collective-permute-start | bytes 98312 | tf_op jit(solution)/shard_map/ppermute | solution.py:25
  440.5 1.9 collective-permute-start.26
  443.7 1.8 collective-permute-done.25
  445.5 2.9 collective-permute-done.26
  449.2 8.2 %constant_dynamic-update-slice_fusion.39 = (f32[24,4,128]{2,1,0:T(4,128)S(1)}, f32[8,4,128]{2,1,0:T(4,128)S(1)}) fusion(f32[8,4,128]{2,1,0:T(4,128)S(1)} %get-tuple-element.18, f32[8,14,4,128]{3,2,1,0:T(4,128)S(1)} %bitcast.437, f32[1,1,8,14,128,128]{5,4,3,2,1,0:T(8,128)} %param.16, f32[8,128]{1,0:T(8,128)S(1)} %bitcast.450, ...), kind=kOutput, calls=%fused_computation.128 | convolution fusion | flops 88104960 | bytes 7639040 | tf_op jit(solution)/shard_map/bkij,bkrj->bri/dot_general | solution.py:51
  459.3 5.6 %collective-permute-start.31 = (f32[1,1,4,4,4,128]{5,4,3,2,1,0:T(4,128)S(1)}, f32[1,1,4,4,4,128]{5,4,3,2,1,0:T(4,128)S(1)}, u32[]{:S(2)}, u32[]{:S(2)}) collective-permute-start(f32[1,1,4,4,4,128]{5,4,3,2,1,0:T(4,128)S(1)} %bitcast.465), channel_id=1, source_target_pairs={{1,0},{2,1},{3,2},{4,3},{5,4},{6,5},{7,6},{8,7},{9,8},{10,9},{11,1... | collective-permute-start | bytes 98312 | tf_op jit(solution)/shard_map/ppermute | solution.py:25
  464.9 1.9 collective-permute-start.30
  469.9 2.9 collective-permute-done.30
  473.5 8.8 %fusion.43 = f32[1,1,8,4,128]{4,3,2,1,0:T(4,128)} fusion(f32[8,4,128]{2,1,0:T(4,128)S(1)} %get-tuple-element.20, f32[8,14,4,128]{3,2,1,0:T(4,128)S(1)} %bitcast.439, f32[1,1,8,14,128,128]{5,4,3,2,1,0:T(8,128)} %param.16, f32[1,1,8,4,128]{4,3,2,1,0:T(4,128)S(1)} %copy-done.4, f32[8,128]{1,0:T(8,128)S(1)} %bitcast.451), kind=kOutput, calls=%fused_computation.43 | convolution fusion | flops 88104960 | bytes 7622656 | tf_op jit(solution)/shard_map/bkij,bkrj->bri/dot_general | solution.py:51
  (145 shorter events, 54.1 us)
Async XLA Ops:
  6.5 83.8 %copy-start = (f32[1,1,2,14,128,128]{5,4,3,2,1,0:T(8,128)S(1)}, f32[1,1,2,14,128,128]{5,4,3,2,1,0:T(8,128)}, u32[]{:S(2)}) copy-start(f32[1,1,2,14,128,128]{5,4,3,2,1,0:T(8,128)} %param.22) | copy-start | bytes 5505028
  6.5 48.1 %copy-start.4 = (f32[1,1,8,4,128]{4,3,2,1,0:T(4,128)S(1)}, f32[1,1,8,4,128]{4,3,2,1,0:T(4,128)}, u32[]{:S(2)}) copy-start(f32[1,1,8,4,128]{4,3,2,1,0:T(4,128)} %param.14) | copy-start | bytes 49156
  6.5 32.0 %copy-start.12 = (s32[1,1,2,14]{3,2,1,0:T(2,128)S(1)}, s32[1,1,2,14]{3,2,1,0:T(2,128)}, u32[]{:S(2)}) copy-start(s32[1,1,2,14]{3,2,1,0:T(2,128)} %param.23) | copy-start | bytes 340
  6.5 157.5 %all-reduce.5.cloned.1.call-start = ((), (), s32[]{:S(2)}) async-start(), calls=%async_computation | async-start | bytes 262144 | tf_op jit(solution)/shard_map/psum | solution.py:37
  8.9 44.2 %copy-start.10 = (s32[1024]{0:T(1024)}, s32[1024]{0:T(1024)S(1)}, u32[]{:S(2)}) copy-start(s32[1024]{0:T(1024)S(1)} %get-tuple-element.22) | copy-start | bytes 12292
  10.3 15.6 %collective-permute-start.3 = (f32[1,1,4,4,4,128]{5,4,3,2,1,0:T(4,128)S(1)}, f32[1,1,4,4,4,128]{5,4,3,2,1,0:T(4,128)S(1)}, u32[]{:S(2)}, u32[]{:S(2)}) collective-permute-start(f32[1,1,4,4,4,128]{5,4,3,2,1,0:T(4,128)S(1)} %bitcast.456), channel_id=1, source_target_pairs={{1,0},{2,1},{3,2},{4,3},{5,4},{6,5},{7,6},{8,7},{9,8},{10,9},{11,1... | collective-permute-start | bytes 98312 | tf_op jit(solution)/shard_map/ppermute | solution.py:25
  17.9 7.9 %collective-permute-start.2 = (f32[1,1,4,4,4,128]{5,4,3,2,1,0:T(4,128)S(1)}, f32[1,1,4,4,4,128]{5,4,3,2,1,0:T(4,128)S(1)}, u32[]{:S(2)}, u32[]{:S(2)}) collective-permute-start(f32[1,1,4,4,4,128]{5,4,3,2,1,0:T(4,128)S(1)} %bitcast.457), channel_id=1, source_target_pairs={{0,1},{1,2},{2,3},{3,4},{4,5},{5,6},{6,7},{7,8},{8,9},{9,10},{10,1... | collective-permute-start | bytes 98312 | tf_op jit(solution)/shard_map/ppermute | solution.py:24
  19.8 5.2 %collective-permute-start.1 = (f32[1,1,4,4,4,128]{5,4,3,2,1,0:T(4,128)S(1)}, f32[1,1,4,4,4,128]{5,4,3,2,1,0:T(4,128)S(1)}, u32[]{:S(2)}, u32[]{:S(2)}) collective-permute-start(f32[1,1,4,4,4,128]{5,4,3,2,1,0:T(4,128)S(1)} %bitcast.458), channel_id=1, source_target_pairs={{32,0},{64,32},{96,64},{128,96},{160,128},{192,160},{224,192},{33,... | collective-permute-start | bytes 98312 | tf_op jit(solution)/shard_map/ppermute | solution.py:25
  21.1 3.9 collective-permute-start
  25.0 28.2 %copy-start.8 = (s32[1024]{0:T(1024)}, s32[1024]{0:T(1024)S(1)}, u32[]{:S(2)}) copy-start(s32[1024]{0:T(1024)S(1)} %pad_clamp_fusion.2) | copy-start | bytes 12292
  26.6 37.2 %copy-start.1 = (f32[1,1,8,128,128]{4,3,2,1,0:T(8,128)S(1)}, f32[1,1,8,128,128]{4,3,2,1,0:T(8,128)}, u32[]{:S(2)}) copy-start(f32[1,1,8,128,128]{4,3,2,1,0:T(8,128)} %param.19) | copy-start | bytes 1572868
  34.9 18.3 %copy-start.5 = (f32[8,4,128]{2,1,0:T(4,128)}, f32[8,4,128]{2,1,0:T(4,128)S(1)}, u32[]{:S(2)}) copy-start(f32[8,4,128]{2,1,0:T(4,128)S(1)} %get-tuple-element.10) | copy-start | bytes 49156
  34.9 286.3 %copy-start.2 = (f32[32,8192]{1,0:T(8,128)S(1)}, f32[32,8192]{1,0:T(8,128)}, u32[]{:S(2)}) copy-start(f32[32,8192]{1,0:T(8,128)} %param.27) | copy-start | bytes 3145732
  35.5 12.9 %collective-permute-start.4 = (f32[1,1,4,4,4,128]{5,4,3,2,1,0:T(4,128)S(1)}, f32[1,1,4,4,4,128]{5,4,3,2,1,0:T(4,128)}, u32[]{:S(2)}, u32[]{:S(2)}) collective-permute-start(f32[1,1,4,4,4,128]{5,4,3,2,1,0:T(4,128)S(1)} %bitcast.460), channel_id=1, source_target_pairs={{0,32},{32,64},{64,96},{96,128},{128,160},{160,192},{192,224},{1,3... | collective-permute-start | bytes 98312 | tf_op jit(solution)/shard_map/ppermute | solution.py:24
  39.2 14.0 %collective-permute-start.7 = (f32[1,1,4,4,4,128]{5,4,3,2,1,0:T(4,128)S(1)}, f32[1,1,4,4,4,128]{5,4,3,2,1,0:T(4,128)S(1)}, u32[]{:S(2)}, u32[]{:S(2)}) collective-permute-start(f32[1,1,4,4,4,128]{5,4,3,2,1,0:T(4,128)S(1)} %bitcast.461), channel_id=1, source_target_pairs={{1,0},{2,1},{3,2},{4,3},{5,4},{6,5},{7,6},{8,7},{9,8},{10,9},{11,1... | collective-permute-start | bytes 98312 | tf_op jit(solution)/shard_map/ppermute | solution.py:25
  45.2 7.9 %collective-permute-start.6 = (f32[1,1,4,4,4,128]{5,4,3,2,1,0:T(4,128)S(1)}, f32[1,1,4,4,4,128]{5,4,3,2,1,0:T(4,128)S(1)}, u32[]{:S(2)}, u32[]{:S(2)}) collective-permute-start(f32[1,1,4,4,4,128]{5,4,3,2,1,0:T(4,128)S(1)} %bitcast.462), channel_id=1, source_target_pairs={{0,1},{1,2},{2,3},{3,4},{4,5},{5,6},{6,7},{7,8},{8,9},{9,10},{10,1... | collective-permute-start | bytes 98312 | tf_op jit(solution)/shard_map/ppermute | solution.py:24
  47.1 4.1 collective-permute-start.5
  54.6 62.6 %copy-start.3 = (f32[1,1,2,128,128]{4,3,2,1,0:T(8,128)S(1)}, f32[1,1,2,128,128]{4,3,2,1,0:T(8,128)}, u32[]{:S(2)}) copy-start(f32[1,1,2,128,128]{4,3,2,1,0:T(8,128)} %param.25) | copy-start | bytes 393220
  69.7 12.9 %collective-permute-start.8 = (f32[1,1,4,2,4,128]{5,4,3,2,1,0:T(4,128)S(1)}, f32[1,1,4,2,4,128]{5,4,3,2,1,0:T(4,128)S(1)}, u32[]{:S(2)}, u32[]{:S(2)}) collective-permute-start(f32[1,1,4,2,4,128]{5,4,3,2,1,0:T(4,128)S(1)} %copy.98), channel_id=1, source_target_pairs={{0,32},{32,64},{64,96},{96,128},{128,160},{160,192},{192,224},{1,3... | collective-permute-start | bytes 49160 | tf_op jit(solution)/shard_map/ppermute | solution.py:24
  73.6 14.1 %collective-permute-start.11 = (f32[1,1,4,2,4,128]{5,4,3,2,1,0:T(4,128)S(1)}, f32[1,1,4,2,4,128]{5,4,3,2,1,0:T(4,128)S(1)}, u32[]{:S(2)}, u32[]{:S(2)}) collective-permute-start(f32[1,1,4,2,4,128]{5,4,3,2,1,0:T(4,128)S(1)} %copy.98), channel_id=1, source_target_pairs={{1,0},{2,1},{3,2},{4,3},{5,4},{6,5},{7,6},{8,7},{9,8},{10,9},{11,1... | collective-permute-start | bytes 49160 | tf_op jit(solution)/shard_map/ppermute | solution.py:25
  79.3 7.7 %collective-permute-start.10 = (f32[1,1,4,2,4,128]{5,4,3,2,1,0:T(4,128)S(1)}, f32[1,1,4,2,4,128]{5,4,3,2,1,0:T(4,128)S(1)}, u32[]{:S(2)}, u32[]{:S(2)}) collective-permute-start(f32[1,1,4,2,4,128]{5,4,3,2,1,0:T(4,128)S(1)} %copy.98), channel_id=1, source_target_pairs={{0,1},{1,2},{2,3},{3,4},{4,5},{5,6},{6,7},{7,8},{8,9},{9,10},{10,1... | collective-permute-start | bytes 49160 | tf_op jit(solution)/shard_map/ppermute | solution.py:24
  81.2 3.1 collective-permute-start.9
  96.1 11.1 %collective-permute-start.12 = (f32[1,1,4,2,4,128]{5,4,3,2,1,0:T(4,128)S(1)}, f32[1,1,4,2,4,128]{5,4,3,2,1,0:T(4,128)S(1)}, u32[]{:S(2)}, u32[]{:S(2)}) collective-permute-start(f32[1,1,4,2,4,128]{5,4,3,2,1,0:T(4,128)S(1)} %copy.104), channel_id=1, source_target_pairs={{0,32},{32,64},{64,96},{96,128},{128,160},{160,192},{192,224},{1,3... | collective-permute-start | bytes 49160 | tf_op jit(solution)/shard_map/ppermute | solution.py:24
  98.0 14.1 %collective-permute-start.15 = (f32[1,1,4,2,4,128]{5,4,3,2,1,0:T(4,128)S(1)}, f32[1,1,4,2,4,128]{5,4,3,2,1,0:T(4,128)S(1)}, u32[]{:S(2)}, u32[]{:S(2)}) collective-permute-start(f32[1,1,4,2,4,128]{5,4,3,2,1,0:T(4,128)S(1)} %copy.104), channel_id=1, source_target_pairs={{1,0},{2,1},{3,2},{4,3},{5,4},{6,5},{7,6},{8,7},{9,8},{10,9},{11,1... | collective-permute-start | bytes 49160 | tf_op jit(solution)/shard_map/ppermute | solution.py:25
  103.7 7.7 %collective-permute-start.14 = (f32[1,1,4,2,4,128]{5,4,3,2,1,0:T(4,128)S(1)}, f32[1,1,4,2,4,128]{5,4,3,2,1,0:T(4,128)S(1)}, u32[]{:S(2)}, u32[]{:S(2)}) collective-permute-start(f32[1,1,4,2,4,128]{5,4,3,2,1,0:T(4,128)S(1)} %copy.104), channel_id=1, source_target_pairs={{0,1},{1,2},{2,3},{3,4},{4,5},{5,6},{6,7},{7,8},{8,9},{9,10},{10,1... | collective-permute-start | bytes 49160 | tf_op jit(solution)/shard_map/ppermute | solution.py:24
  105.7 3.1 collective-permute-start.13
  119.2 76.6 %all-reduce.7.cloned.1.call-start = ((), (), s32[]{:S(2)}) async-start(), calls=%async_computation.1 | async-start | bytes 262144 | tf_op jit(solution)/shard_map/psum | solution.py:37
  164.0 80.8 %all-reduce.9.cloned.1.call-start = ((), (), s32[]{:S(2)}) async-start(), calls=%async_computation.2 | async-start | bytes 262144 | tf_op jit(solution)/shard_map/psum | solution.py:37
  195.8 125.3 %all-reduce.11.cloned.1.call-start = ((), (), s32[]{:S(2)}) async-start(), calls=%async_computation.3 | async-start | bytes 262144 | tf_op jit(solution)/shard_map/psum | solution.py:37
  323.0 109.8 %copy-start.11 = (s32[1024]{0:T(1024)S(1)}, s32[1024]{0:T(1024)}, u32[]{:S(2)}) copy-start(s32[1024]{0:T(1024)} %copy-done.10) | copy-start | bytes 12292
  323.0 125.4 %copy-start.9 = (s32[1024]{0:T(1024)S(1)}, s32[1024]{0:T(1024)}, u32[]{:S(2)}) copy-start(s32[1024]{0:T(1024)} %copy-done.8) | copy-start | bytes 12292
  323.0 126.2 %copy-start.7 = (f32[1,1,8,128]{3,2,1,0:T(8,128)S(1)}, f32[1,1,8,128]{3,2,1,0:T(8,128)}, u32[]{:S(2)}) copy-start(f32[1,1,8,128]{3,2,1,0:T(8,128)} %param.15) | copy-start | bytes 12292
  395.9 9.1 %collective-permute-start.16 = (f32[1,1,4,2,4,128]{5,4,3,2,1,0:T(4,128)S(1)}, f32[1,1,4,2,4,128]{5,4,3,2,1,0:T(4,128)S(1)}, u32[]{:S(2)}, u32[]{:S(2)}) collective-permute-start(f32[1,1,4,2,4,128]{5,4,3,2,1,0:T(4,128)S(1)} %copy.113), channel_id=1, source_target_pairs={{0,32},{32,64},{64,96},{96,128},{128,160},{160,192},{192,224},{1,3... | collective-permute-start | bytes 49160 | tf_op jit(solution)/shard_map/ppermute | solution.py:24
  397.2 12.4 %collective-permute-start.19 = (f32[1,1,4,2,4,128]{5,4,3,2,1,0:T(4,128)S(1)}, f32[1,1,4,2,4,128]{5,4,3,2,1,0:T(4,128)S(1)}, u32[]{:S(2)}, u32[]{:S(2)}) collective-permute-start(f32[1,1,4,2,4,128]{5,4,3,2,1,0:T(4,128)S(1)} %copy.113), channel_id=1, source_target_pairs={{1,0},{2,1},{3,2},{4,3},{5,4},{6,5},{7,6},{8,7},{9,8},{10,9},{11,1... | collective-permute-start | bytes 49160 | tf_op jit(solution)/shard_map/ppermute | solution.py:25
  401.8 7.7 %collective-permute-start.18 = (f32[1,1,4,2,4,128]{5,4,3,2,1,0:T(4,128)S(1)}, f32[1,1,4,2,4,128]{5,4,3,2,1,0:T(4,128)S(1)}, u32[]{:S(2)}, u32[]{:S(2)}) collective-permute-start(f32[1,1,4,2,4,128]{5,4,3,2,1,0:T(4,128)S(1)} %copy.113), channel_id=1, source_target_pairs={{0,1},{1,2},{2,3},{3,4},{4,5},{5,6},{6,7},{7,8},{8,9},{9,10},{10,1... | collective-permute-start | bytes 49160 | tf_op jit(solution)/shard_map/ppermute | solution.py:24
  403.7 3.1 collective-permute-start.17
  413.3 9.5 %collective-permute-start.20 = (f32[1,1,4,2,4,128]{5,4,3,2,1,0:T(4,128)S(1)}, f32[1,1,4,2,4,128]{5,4,3,2,1,0:T(4,128)S(1)}, u32[]{:S(2)}, u32[]{:S(2)}) collective-permute-start(f32[1,1,4,2,4,128]{5,4,3,2,1,0:T(4,128)S(1)} %copy.119), channel_id=1, source_target_pairs={{0,32},{32,64},{64,96},{96,128},{128,160},{160,192},{192,224},{1,3... | collective-permute-start | bytes 49160 | tf_op jit(solution)/shard_map/ppermute | solution.py:24
  414.6 12.7 %collective-permute-start.23 = (f32[1,1,4,2,4,128]{5,4,3,2,1,0:T(4,128)S(1)}, f32[1,1,4,2,4,128]{5,4,3,2,1,0:T(4,128)S(1)}, u32[]{:S(2)}, u32[]{:S(2)}) collective-permute-start(f32[1,1,4,2,4,128]{5,4,3,2,1,0:T(4,128)S(1)} %copy.119), channel_id=1, source_target_pairs={{1,0},{2,1},{3,2},{4,3},{5,4},{6,5},{7,6},{8,7},{9,8},{10,9},{11,1... | collective-permute-start | bytes 49160 | tf_op jit(solution)/shard_map/ppermute | solution.py:25
  419.5 7.7 %collective-permute-start.22 = (f32[1,1,4,2,4,128]{5,4,3,2,1,0:T(4,128)S(1)}, f32[1,1,4,2,4,128]{5,4,3,2,1,0:T(4,128)S(1)}, u32[]{:S(2)}, u32[]{:S(2)}) collective-permute-start(f32[1,1,4,2,4,128]{5,4,3,2,1,0:T(4,128)S(1)} %copy.119), channel_id=1, source_target_pairs={{0,1},{1,2},{2,3},{3,4},{4,5},{5,6},{6,7},{7,8},{8,9},{9,10},{10,1... | collective-permute-start | bytes 49160 | tf_op jit(solution)/shard_map/ppermute | solution.py:24
  421.4 3.1 collective-permute-start.21
  433.4 10.3 %collective-permute-start.24 = (f32[1,1,4,4,4,128]{5,4,3,2,1,0:T(4,128)S(1)}, f32[1,1,4,4,4,128]{5,4,3,2,1,0:T(4,128)S(1)}, u32[]{:S(2)}, u32[]{:S(2)}) collective-permute-start(f32[1,1,4,4,4,128]{5,4,3,2,1,0:T(4,128)S(1)} %bitcast.468), channel_id=1, source_target_pairs={{0,32},{32,64},{64,96},{96,128},{128,160},{160,192},{192,224},{1,3... | collective-permute-start | bytes 98312 | tf_op jit(solution)/shard_map/ppermute | solution.py:24
  434.7 13.7 %collective-permute-start.27 = (f32[1,1,4,4,4,128]{5,4,3,2,1,0:T(4,128)S(1)}, f32[1,1,4,4,4,128]{5,4,3,2,1,0:T(4,128)S(1)}, u32[]{:S(2)}, u32[]{:S(2)}) collective-permute-start(f32[1,1,4,4,4,128]{5,4,3,2,1,0:T(4,128)S(1)} %bitcast.469), channel_id=1, source_target_pairs={{1,0},{2,1},{3,2},{4,3},{5,4},{6,5},{7,6},{8,7},{9,8},{10,9},{11,1... | collective-permute-start | bytes 98312 | tf_op jit(solution)/shard_map/ppermute | solution.py:25
  440.5 7.9 %collective-permute-start.26 = (f32[1,1,4,4,4,128]{5,4,3,2,1,0:T(4,128)S(1)}, f32[1,1,4,4,4,128]{5,4,3,2,1,0:T(4,128)S(1)}, u32[]{:S(2)}, u32[]{:S(2)}) collective-permute-start(f32[1,1,4,4,4,128]{5,4,3,2,1,0:T(4,128)S(1)} %bitcast.470), channel_id=1, source_target_pairs={{0,1},{1,2},{2,3},{3,4},{4,5},{5,6},{6,7},{7,8},{8,9},{9,10},{10,1... | collective-permute-start | bytes 98312 | tf_op jit(solution)/shard_map/ppermute | solution.py:24
  442.4 3.1 collective-permute-start.25
  458.0 10.3 %collective-permute-start.28 = (f32[1,1,4,4,4,128]{5,4,3,2,1,0:T(4,128)S(1)}, f32[1,1,4,4,4,128]{5,4,3,2,1,0:T(4,128)S(1)}, u32[]{:S(2)}, u32[]{:S(2)}) collective-permute-start(f32[1,1,4,4,4,128]{5,4,3,2,1,0:T(4,128)S(1)} %bitcast.464), channel_id=1, source_target_pairs={{0,32},{32,64},{64,96},{96,128},{128,160},{160,192},{192,224},{1,3... | collective-permute-start | bytes 98312 | tf_op jit(solution)/shard_map/ppermute | solution.py:24
  459.3 13.5 %collective-permute-start.31 = (f32[1,1,4,4,4,128]{5,4,3,2,1,0:T(4,128)S(1)}, f32[1,1,4,4,4,128]{5,4,3,2,1,0:T(4,128)S(1)}, u32[]{:S(2)}, u32[]{:S(2)}) collective-permute-start(f32[1,1,4,4,4,128]{5,4,3,2,1,0:T(4,128)S(1)} %bitcast.465), channel_id=1, source_target_pairs={{1,0},{2,1},{3,2},{4,3},{5,4},{6,5},{7,6},{8,7},{9,8},{10,9},{11,1... | collective-permute-start | bytes 98312 | tf_op jit(solution)/shard_map/ppermute | solution.py:25
  464.9 7.9 %collective-permute-start.30 = (f32[1,1,4,4,4,128]{5,4,3,2,1,0:T(4,128)S(1)}, f32[1,1,4,4,4,128]{5,4,3,2,1,0:T(4,128)S(1)}, u32[]{:S(2)}, u32[]{:S(2)}) collective-permute-start(f32[1,1,4,4,4,128]{5,4,3,2,1,0:T(4,128)S(1)} %bitcast.466), channel_id=1, source_target_pairs={{0,1},{1,2},{2,3},{3,4},{4,5},{5,6},{6,7},{7,8},{8,9},{9,10},{10,1... | collective-permute-start | bytes 98312 | tf_op jit(solution)/shard_map/ppermute | solution.py:24
  466.8 3.1 collective-permute-start.29
  (1 other events, 0.6 us)
Sparse Core Ops, SparseCore 0:
  119.3 44.6 all-reduce.4
  166.6 29.1 all-reduce.6
  198.1 46.6 all-reduce.8
  247.0 74.1 all-reduce.10
where the time goes:
time: 491 us; the launch traced here: 489 us
  waiting for transfers between devices  231 us (47%)
  starting transfers between devices  87.9 us (18%)
  blocking collectives  70 us (14%)
  matrix products  53.4 us (11%)
  local copies, waits for them, and re-layouts  26.7 us (5%)
  between operations  13.6 us (3%)
  other arithmetic  6.11 us (1%)
    psum x4, waiting for transfers between devices, by_axis(): return functools.reduce(lax.psum, axes, value)  202 us
    all_gather x1, blocking collectives, on_device(): coarse_x = lax.all_gather(own_rows, ROW_COL, axis=1, tiled=True)  70 us
    ppermute x16, starting transfers between devices, extended_2(): lax.ppermute(leading, axis, [(b, a) for a, b in up])  56.7 us
    dot_general x8, matrix products, apply_op(): coupled = jnp.einsum('bkij,bkrj->bri', blocks, nearby, precision=HIGH)  44.6 us
    ppermute x16, starting transfers between devices, extended_2(): lax.ppermute(last, axis, up)  31.1 us
    ppermute x16, waiting for transfers between devices, extended_2(): lax.ppermute(last, axis, up)  18.3 us
    ppermute x16, waiting for transfers between devices, extended_2(): lax.ppermute(leading, axis, [(b, a) for a, b in up])  11.1 us
  transfers between devices with their start and end apart: 36, of which 19 were waited for; matrix products, arithmetic and copies ran while one was open for 1% of the time, Pallas kernels for 0%

commit v1 on v0

--- a/solution.py
+++ b/solution.py
@@ -94,7 +94,9 @@
     term = jnp.einsum("bc,brj->rcj", onehot1, contrib, precision=HIGH).reshape(loads, coarse_total)
     coarse_rhs = by_axis(term, ROW_COL)
     own_rows = jnp.einsum("ij,rj->ri", cinv, coarse_rhs, precision=HIGH)
-    coarse_x = lax.all_gather(own_rows, ROW_COL, axis=1, tiled=True)
+    coarse_x = jnp.concatenate(
+        lax.all_to_all(jnp.stack([own_rows] * lax.axis_size(ROW_COL)), ROW_COL, 0, 0), axis=1
+    )
     coarse_blocks = coarse_x.reshape(loads, coarse_count, block_size)
     picked = jnp.einsum("bc,rcj->brj", onehot1, coarse_blocks, precision=HIGH)
     level_x = level_x + jnp.einsum("bij,brj->bri", level_pro, picked, precision=HIGH)

time: 491 us -> 445 us (0.906)
  blocking collectives: 70 us -> 22.2 us
    all_gather x1 -> x0, blocking collectives: 70 us -> none  [on_device(): coarse_x = lax.all_gather(own_rows, ROW_COL, axis=1, tiled=True)]
    all_to_all x0 -> x1, blocking collectives: none -> 22.2 us  [on_device(): lax.all_to_all(jnp.stack([own_rows] * lax.axis_size(ROW_COL)), ROW_COL, 0...]
  transfers between devices with their start and end apart: 36 -> 36, of which waited for: 19 -> 19; matrix products, arithmetic and copies ran while one was open for 1% -> 2% of each run, Pallas kernels for 0% -> 0%
where the time goes in v1:
time: 445 us; the launch traced here: 443 us
  waiting for transfers between devices  230 us (52%)
  starting transfers between devices  88.9 us (20%)
  matrix products  53.4 us (12%)
  local copies, waits for them, and re-layouts  28 us (6%)
  blocking collectives  22.2 us (5%)
  between operations  13.7 us (3%)
  other arithmetic  7 us (2%)
    psum x4, waiting for transfers between devices, by_axis(): return functools.reduce(lax.psum, axes, value)  202 us
    ppermute x16, starting transfers between devices, extended_2(): lax.ppermute(leading, axis, [(b, a) for a, b in up])  54.9 us
    dot_general x8, matrix products, apply_op(): coupled = jnp.einsum('bkij,bkrj->bri', blocks, nearby, precision=HIGH)  44.7 us
    ppermute x16, starting transfers between devices, extended_2(): lax.ppermute(last, axis, up)  33.9 us
    all_to_all x1, blocking collectives, on_device(): lax.all_to_all(jnp.stack([own_rows] * lax.axis_size(ROW_COL)), ROW_COL, 0...  22.2 us
    ppermute x16, waiting for transfers between devices, extended_2(): lax.ppermute(last, axis, up)  17.2 us
    ppermute x16, waiting for transfers between devices, extended_2(): lax.ppermute(leading, axis, [(b, a) for a, b in up])  11.1 us
    gather x12, local copies, waits for them, and re-layouts, gather_ghosts(): packed = vector[sends]  9.3 us
  transfers between devices with their start and end apart: 36, of which 19 were waited for; matrix products, arithmetic and copies ran while one was open for 2% of the time, Pallas kernels for 0%

profile of v1, /device:TPU:8, one launch (start us, length us, event | category | flops | bytes accessed | tf_op | source)
XLA Modules:
  0.0 443.4 jit_solution(13891947544888071292)
XLA Ops:
  10.3 7.6 %collective-permute-start.3 = (f32[1,1,4,4,4,128]{5,4,3,2,1,0:T(4,128)S(1)}, f32[1,1,4,4,4,128]{5,4,3,2,1,0:T(4,128)S(1)}, u32[]{:S(2)}, u32[]{:S(2)}) collective-permute-start(f32[1,1,4,4,4,128]{5,4,3,2,1,0:T(4,128)S(1)} %bitcast.447), channel_id=1, source_target_pairs={{1,0},{2,1},{3,2},{4,3},{5,4},{6,5},{7,6},{8,7},{9,8},{10,9},{11,1... | collective-permute-start | bytes 98312 | tf_op jit(solution)/shard_map/ppermute | solution.py:25
  17.9 1.9 collective-permute-start.2
  21.1 3.0 collective-permute-start
  26.6 8.3 %constant_dynamic-update-slice_fusion.9 = (f32[24,4,128]{2,1,0:T(4,128)S(1)}, f32[8,4,128]{2,1,0:T(4,128)S(1)}) fusion(f32[8,14,4,128]{3,2,1,0:T(4,128)S(1)} %bitcast.430, f32[1,1,8,14,128,128]{5,4,3,2,1,0:T(8,128)} %param.16, f32[8,128]{1,0:T(8,128)} %bitcast.439, f32[1,1,8,4,128]{4,3,2,1,0:T(4,128)} %param.14), kind=kOutput, calls=%fused_computation.94 | convolution fusion | flops 88113152 | bytes 7622656 | tf_op jit(solution)/shard_map/bkij,bkrj->bri/dot_general | solution.py:51
  35.5 3.0 collective-permute-start.4
  39.1 6.0 %collective-permute-start.7 = (f32[1,1,4,4,4,128]{5,4,3,2,1,0:T(4,128)S(1)}, f32[1,1,4,4,4,128]{5,4,3,2,1,0:T(4,128)S(1)}, u32[]{:S(2)}, u32[]{:S(2)}) collective-permute-start(f32[1,1,4,4,4,128]{5,4,3,2,1,0:T(4,128)S(1)} %bitcast.452), channel_id=1, source_target_pairs={{1,0},{2,1},{3,2},{4,3},{5,4},{6,5},{7,6},{8,7},{9,8},{10,9},{11,1... | collective-permute-start | bytes 98312 | tf_op jit(solution)/shard_map/ppermute | solution.py:25
  45.2 1.9 collective-permute-start.6
  49.1 2.0 collective-permute-done.5
  51.2 1.9 collective-permute-done.6
  54.5 9.2 %fusion.64 = f32[8,4,128]{2,1,0:T(4,128)S(1)} fusion(f32[8,14,4,128]{3,2,1,0:T(4,128)} %bitcast.432, f32[1,1,8,14,128,128]{5,4,3,2,1,0:T(8,128)} %param.16, f32[1,1,8,4,128]{4,3,2,1,0:T(4,128)S(1)} %copy-done.4, f32[8,4,128]{2,1,0:T(4,128)} %copy-done.5, f32[8,128]{1,0:T(8,128)} %bitcast.440), kind=kOutput, calls=%fused_computation.50 | convolution fusion | flops 88092672 | bytes 7622656 | tf_op jit(solution)/shard_map/bkij,bkrj->bri/dot_general | solution.py:51
  67.0 2.0 gather_fusion.4
  69.7 2.6 collective-permute-start.8
  73.5 5.7 %collective-permute-start.11 = (f32[1,1,4,2,4,128]{5,4,3,2,1,0:T(4,128)S(1)}, f32[1,1,4,2,4,128]{5,4,3,2,1,0:T(4,128)S(1)}, u32[]{:S(2)}, u32[]{:S(2)}) collective-permute-start(f32[1,1,4,2,4,128]{5,4,3,2,1,0:T(4,128)S(1)} %copy.97), channel_id=1, source_target_pairs={{1,0},{2,1},{3,2},{4,3},{5,4},{6,5},{7,6},{8,7},{9,8},{10,9},{11,1... | collective-permute-start | bytes 49160 | tf_op jit(solution)/shard_map/ppermute | solution.py:25
  79.3 1.9 collective-permute-start.10
  84.9 2.1 collective-permute-done.10
  88.2 2.1 gather_fusion.5
  90.2 3.1 constant_dynamic-update-slice_fusion.19
  93.3 2.0 gather_fusion.6
  96.0 1.9 collective-permute-start.12
  97.9 5.7 %collective-permute-start.15 = (f32[1,1,4,2,4,128]{5,4,3,2,1,0:T(4,128)S(1)}, f32[1,1,4,2,4,128]{5,4,3,2,1,0:T(4,128)S(1)}, u32[]{:S(2)}, u32[]{:S(2)}) collective-permute-start(f32[1,1,4,2,4,128]{5,4,3,2,1,0:T(4,128)S(1)} %copy.103), channel_id=1, source_target_pairs={{1,0},{2,1},{3,2},{4,3},{5,4},{6,5},{7,6},{8,7},{9,8},{10,9},{11,1... | collective-permute-start | bytes 49160 | tf_op jit(solution)/shard_map/ppermute | solution.py:25
  103.6 1.9 collective-permute-start.14
  109.3 2.1 collective-permute-done.14
  112.6 2.1 gather_fusion.7
  114.6 2.4 fusion.127
  119.1 44.8 %all-reduce.5.cloned.1.call-done = f32[4,8192]{1,0:T(4,128)} async-done(((f32[4,8192]{1,0:T(4,128)}), f32[4,8192]{1,0:T(4,128)}) %all-reduce.5.cloned.1.call-update) | async-done | bytes 131088 | tf_op jit(solution)/shard_map/psum | solution.py:37
  164.0 31.7 %all-reduce.7.cloned.1.call-done = f32[4,8192]{1,0:T(4,128)} async-done(((f32[4,8192]{1,0:T(4,128)}), f32[4,8192]{1,0:T(4,128)}) %all-reduce.7.cloned.1.call-update) | async-done | bytes 131088 | tf_op jit(solution)/shard_map/psum | solution.py:37
  195.8 49.0 %all-reduce.9.cloned.1.call-done = f32[4,8192]{1,0:T(4,128)} async-done(((f32[4,8192]{1,0:T(4,128)}), f32[4,8192]{1,0:T(4,128)}) %all-reduce.9.cloned.1.call-update) | async-done | bytes 131088 | tf_op jit(solution)/shard_map/psum | solution.py:37
  244.7 76.3 %all-reduce.11.cloned.1.call-done = f32[4,8192]{1,0:T(4,128)} async-done(((f32[4,8192]{1,0:T(4,128)}), f32[4,8192]{1,0:T(4,128)}) %all-reduce.11.cloned.1.call-update) | async-done | bytes 131088 | tf_op jit(solution)/shard_map/psum | solution.py:37
  321.1 1.8 fusion.168
  323.3 22.2 %all_to_all.5 = f32[256,1,128]{2,1,0:T(1,128)S(1)} all-to-all(f32[256,1,128]{2,1,0:T(1,128)S(1)} %reshape.288), channel_id=1, replica_groups=mesh['row_0'=4,'row_1'=2,'col_0'=4,'col_1'=8] {'row_0','row_1','col_0','..., dimensions={0} | all-to-all | bytes 262144 | tf_op jit(solution)/shard_map/all_to_all | solution.py:98
  350.1 1.9 collective-permute-start.16
  352.0 2.8 collective-permute-start.19
  354.8 3.1 collective-permute-start.18
  363.4 2.3 constant_dynamic-update-slice_fusion.29
  366.4 2.4 collective-permute-start.20
  368.8 5.5 %collective-permute-start.23 = (f32[1,1,4,2,4,128]{5,4,3,2,1,0:T(4,128)S(1)}, f32[1,1,4,2,4,128]{5,4,3,2,1,0:T(4,128)S(1)}, u32[]{:S(2)}, u32[]{:S(2)}) collective-permute-start(f32[1,1,4,2,4,128]{5,4,3,2,1,0:T(4,128)S(1)} %copy.118), channel_id=1, source_target_pairs={{1,0},{2,1},{3,2},{4,3},{5,4},{6,5},{7,6},{8,7},{9,8},{10,9},{11,1... | collective-permute-start | bytes 49160 | tf_op jit(solution)/shard_map/ppermute | solution.py:25
  374.3 1.9 collective-permute-start.22
  379.3 2.7 collective-permute-done.22
  382.8 2.3 fusion.106
  389.6 5.4 %collective-permute-start.27 = (f32[1,1,4,4,4,128]{5,4,3,2,1,0:T(4,128)S(1)}, f32[1,1,4,4,4,128]{5,4,3,2,1,0:T(4,128)S(1)}, u32[]{:S(2)}, u32[]{:S(2)}) collective-permute-start(f32[1,1,4,4,4,128]{5,4,3,2,1,0:T(4,128)S(1)} %bitcast.460), channel_id=1, source_target_pairs={{1,0},{2,1},{3,2},{4,3},{5,4},{6,5},{7,6},{8,7},{9,8},{10,9},{11,1... | collective-permute-start | bytes 98312 | tf_op jit(solution)/shard_map/ppermute | solution.py:25
  395.0 1.9 collective-permute-start.26
  400.0 2.9 collective-permute-done.26
  403.8 8.2 %constant_dynamic-update-slice_fusion.39 = (f32[24,4,128]{2,1,0:T(4,128)S(1)}, f32[8,4,128]{2,1,0:T(4,128)S(1)}) fusion(f32[8,4,128]{2,1,0:T(4,128)S(1)} %get-tuple-element.18, f32[8,14,4,128]{3,2,1,0:T(4,128)S(1)} %bitcast.429, f32[1,1,8,14,128,128]{5,4,3,2,1,0:T(8,128)} %param.16, f32[8,128]{1,0:T(8,128)} %bitcast.441, f32[1,1,8,4,128]{4,3,2,1,0:T(4,128)S(1)} %copy-done.4), kind=kOutput, calls=%fused_computation.124 | convolution fusion | flops 88104960 | bytes 7639040 | tf_op jit(solution)/shard_map/bkij,bkrj->bri/dot_general | solution.py:51
  413.9 5.4 %collective-permute-start.31 = (f32[1,1,4,4,4,128]{5,4,3,2,1,0:T(4,128)S(1)}, f32[1,1,4,4,4,128]{5,4,3,2,1,0:T(4,128)S(1)}, u32[]{:S(2)}, u32[]{:S(2)}) collective-permute-start(f32[1,1,4,4,4,128]{5,4,3,2,1,0:T(4,128)S(1)} %bitcast.456), channel_id=1, source_target_pairs={{1,0},{2,1},{3,2},{4,3},{5,4},{6,5},{7,6},{8,7},{9,8},{10,9},{11,1... | collective-permute-start | bytes 98312 | tf_op jit(solution)/shard_map/ppermute | solution.py:25
  419.3 1.9 collective-permute-start.30
  422.5 1.8 collective-permute-done.29
  424.3 2.9 collective-permute-done.30
  428.0 8.8 %fusion.43 = f32[1,1,8,4,128]{4,3,2,1,0:T(4,128)} fusion(f32[8,4,128]{2,1,0:T(4,128)S(1)} %get-tuple-element.20, f32[8,14,4,128]{3,2,1,0:T(4,128)S(1)} %bitcast.431, f32[1,1,8,14,128,128]{5,4,3,2,1,0:T(8,128)} %param.16, f32[1,1,8,4,128]{4,3,2,1,0:T(4,128)S(1)} %copy-done.4, f32[8,128]{1,0:T(8,128)S(1)} %bitcast.442), kind=kOutput, calls=%fused_computation.43 | convolution fusion | flops 88104960 | bytes 7622656 | tf_op jit(solution)/shard_map/bkij,bkrj->bri/dot_general | solution.py:51
  (150 shorter events, 57.1 us)
Async XLA Ops:
  6.5 83.7 %copy-start = (f32[1,1,2,14,128,128]{5,4,3,2,1,0:T(8,128)S(1)}, f32[1,1,2,14,128,128]{5,4,3,2,1,0:T(8,128)}, u32[]{:S(2)}) copy-start(f32[1,1,2,14,128,128]{5,4,3,2,1,0:T(8,128)} %param.22) | copy-start | bytes 5505028
  6.5 48.0 %copy-start.4 = (f32[1,1,8,4,128]{4,3,2,1,0:T(4,128)S(1)}, f32[1,1,8,4,128]{4,3,2,1,0:T(4,128)}, u32[]{:S(2)}) copy-start(f32[1,1,8,4,128]{4,3,2,1,0:T(4,128)} %param.14) | copy-start | bytes 49156
  6.5 32.0 %copy-start.12 = (s32[1,1,2,14]{3,2,1,0:T(2,128)S(1)}, s32[1,1,2,14]{3,2,1,0:T(2,128)}, u32[]{:S(2)}) copy-start(s32[1,1,2,14]{3,2,1,0:T(2,128)} %param.23) | copy-start | bytes 340
  6.5 157.4 %all-reduce.5.cloned.1.call-start = ((), (), s32[]{:S(2)}) async-start(), calls=%async_computation.1 | async-start | bytes 262144 | tf_op jit(solution)/shard_map/psum | solution.py:37
  8.9 44.2 %copy-start.10 = (s32[1024]{0:T(1024)}, s32[1024]{0:T(1024)S(1)}, u32[]{:S(2)}) copy-start(s32[1024]{0:T(1024)S(1)} %get-tuple-element.22) | copy-start | bytes 12292
  10.3 15.6 %collective-permute-start.3 = (f32[1,1,4,4,4,128]{5,4,3,2,1,0:T(4,128)S(1)}, f32[1,1,4,4,4,128]{5,4,3,2,1,0:T(4,128)S(1)}, u32[]{:S(2)}, u32[]{:S(2)}) collective-permute-start(f32[1,1,4,4,4,128]{5,4,3,2,1,0:T(4,128)S(1)} %bitcast.447), channel_id=1, source_target_pairs={{1,0},{2,1},{3,2},{4,3},{5,4},{6,5},{7,6},{8,7},{9,8},{10,9},{11,1... | collective-permute-start | bytes 98312 | tf_op jit(solution)/shard_map/ppermute | solution.py:25
  17.9 7.9 %collective-permute-start.2 = (f32[1,1,4,4,4,128]{5,4,3,2,1,0:T(4,128)S(1)}, f32[1,1,4,4,4,128]{5,4,3,2,1,0:T(4,128)S(1)}, u32[]{:S(2)}, u32[]{:S(2)}) collective-permute-start(f32[1,1,4,4,4,128]{5,4,3,2,1,0:T(4,128)S(1)} %bitcast.448), channel_id=1, source_target_pairs={{0,1},{1,2},{2,3},{3,4},{4,5},{5,6},{6,7},{7,8},{8,9},{9,10},{10,1... | collective-permute-start | bytes 98312 | tf_op jit(solution)/shard_map/ppermute | solution.py:24
  19.8 5.2 %collective-permute-start.1 = (f32[1,1,4,4,4,128]{5,4,3,2,1,0:T(4,128)S(1)}, f32[1,1,4,4,4,128]{5,4,3,2,1,0:T(4,128)S(1)}, u32[]{:S(2)}, u32[]{:S(2)}) collective-permute-start(f32[1,1,4,4,4,128]{5,4,3,2,1,0:T(4,128)S(1)} %bitcast.449), channel_id=1, source_target_pairs={{32,0},{64,32},{96,64},{128,96},{160,128},{192,160},{224,192},{33,... | collective-permute-start | bytes 98312 | tf_op jit(solution)/shard_map/ppermute | solution.py:25
  21.1 3.9 collective-permute-start
  25.0 28.1 %copy-start.8 = (s32[1024]{0:T(1024)}, s32[1024]{0:T(1024)S(1)}, u32[]{:S(2)}) copy-start(s32[1024]{0:T(1024)S(1)} %pad_clamp_fusion.2) | copy-start | bytes 12292
  26.6 37.2 %copy-start.1 = (f32[1,1,8,128,128]{4,3,2,1,0:T(8,128)S(1)}, f32[1,1,8,128,128]{4,3,2,1,0:T(8,128)}, u32[]{:S(2)}) copy-start(f32[1,1,8,128,128]{4,3,2,1,0:T(8,128)} %param.19) | copy-start | bytes 1572868
  34.9 18.2 %copy-start.5 = (f32[8,4,128]{2,1,0:T(4,128)}, f32[8,4,128]{2,1,0:T(4,128)S(1)}, u32[]{:S(2)}) copy-start(f32[8,4,128]{2,1,0:T(4,128)S(1)} %get-tuple-element.10) | copy-start | bytes 49156
  34.9 286.1 %copy-start.2 = (f32[32,8192]{1,0:T(8,128)S(1)}, f32[32,8192]{1,0:T(8,128)}, u32[]{:S(2)}) copy-start(f32[32,8192]{1,0:T(8,128)} %param.27) | copy-start | bytes 3145732
  35.5 12.9 %collective-permute-start.4 = (f32[1,1,4,4,4,128]{5,4,3,2,1,0:T(4,128)S(1)}, f32[1,1,4,4,4,128]{5,4,3,2,1,0:T(4,128)}, u32[]{:S(2)}, u32[]{:S(2)}) collective-permute-start(f32[1,1,4,4,4,128]{5,4,3,2,1,0:T(4,128)S(1)} %bitcast.451), channel_id=1, source_target_pairs={{0,32},{32,64},{64,96},{96,128},{128,160},{160,192},{192,224},{1,3... | collective-permute-start | bytes 98312 | tf_op jit(solution)/shard_map/ppermute | solution.py:24
  39.1 14.0 %collective-permute-start.7 = (f32[1,1,4,4,4,128]{5,4,3,2,1,0:T(4,128)S(1)}, f32[1,1,4,4,4,128]{5,4,3,2,1,0:T(4,128)S(1)}, u32[]{:S(2)}, u32[]{:S(2)}) collective-permute-start(f32[1,1,4,4,4,128]{5,4,3,2,1,0:T(4,128)S(1)} %bitcast.452), channel_id=1, source_target_pairs={{1,0},{2,1},{3,2},{4,3},{5,4},{6,5},{7,6},{8,7},{9,8},{10,9},{11,1... | collective-permute-start | bytes 98312 | tf_op jit(solution)/shard_map/ppermute | solution.py:25
  45.2 7.9 %collective-permute-start.6 = (f32[1,1,4,4,4,128]{5,4,3,2,1,0:T(4,128)S(1)}, f32[1,1,4,4,4,128]{5,4,3,2,1,0:T(4,128)S(1)}, u32[]{:S(2)}, u32[]{:S(2)}) collective-permute-start(f32[1,1,4,4,4,128]{5,4,3,2,1,0:T(4,128)S(1)} %bitcast.453), channel_id=1, source_target_pairs={{0,1},{1,2},{2,3},{3,4},{4,5},{5,6},{6,7},{7,8},{8,9},{9,10},{10,1... | collective-permute-start | bytes 98312 | tf_op jit(solution)/shard_map/ppermute | solution.py:24
  47.1 4.1 collective-permute-start.5
  54.5 62.5 %copy-start.3 = (f32[1,1,2,128,128]{4,3,2,1,0:T(8,128)S(1)}, f32[1,1,2,128,128]{4,3,2,1,0:T(8,128)}, u32[]{:S(2)}) copy-start(f32[1,1,2,128,128]{4,3,2,1,0:T(8,128)} %param.25) | copy-start | bytes 393220
  69.7 12.8 %collective-permute-start.8 = (f32[1,1,4,2,4,128]{5,4,3,2,1,0:T(4,128)S(1)}, f32[1,1,4,2,4,128]{5,4,3,2,1,0:T(4,128)S(1)}, u32[]{:S(2)}, u32[]{:S(2)}) collective-permute-start(f32[1,1,4,2,4,128]{5,4,3,2,1,0:T(4,128)S(1)} %copy.97), channel_id=1, source_target_pairs={{0,32},{32,64},{64,96},{96,128},{128,160},{160,192},{192,224},{1,3... | collective-permute-start | bytes 49160 | tf_op jit(solution)/shard_map/ppermute | solution.py:24
  73.5 14.1 %collective-permute-start.11 = (f32[1,1,4,2,4,128]{5,4,3,2,1,0:T(4,128)S(1)}, f32[1,1,4,2,4,128]{5,4,3,2,1,0:T(4,128)S(1)}, u32[]{:S(2)}, u32[]{:S(2)}) collective-permute-start(f32[1,1,4,2,4,128]{5,4,3,2,1,0:T(4,128)S(1)} %copy.97), channel_id=1, source_target_pairs={{1,0},{2,1},{3,2},{4,3},{5,4},{6,5},{7,6},{8,7},{9,8},{10,9},{11,1... | collective-permute-start | bytes 49160 | tf_op jit(solution)/shard_map/ppermute | solution.py:25
  79.3 7.7 %collective-permute-start.10 = (f32[1,1,4,2,4,128]{5,4,3,2,1,0:T(4,128)S(1)}, f32[1,1,4,2,4,128]{5,4,3,2,1,0:T(4,128)S(1)}, u32[]{:S(2)}, u32[]{:S(2)}) collective-permute-start(f32[1,1,4,2,4,128]{5,4,3,2,1,0:T(4,128)S(1)} %copy.97), channel_id=1, source_target_pairs={{0,1},{1,2},{2,3},{3,4},{4,5},{5,6},{6,7},{7,8},{8,9},{9,10},{10,1... | collective-permute-start | bytes 49160 | tf_op jit(solution)/shard_map/ppermute | solution.py:24
  81.2 3.1 collective-permute-start.9
  96.0 11.1 %collective-permute-start.12 = (f32[1,1,4,2,4,128]{5,4,3,2,1,0:T(4,128)S(1)}, f32[1,1,4,2,4,128]{5,4,3,2,1,0:T(4,128)S(1)}, u32[]{:S(2)}, u32[]{:S(2)}) collective-permute-start(f32[1,1,4,2,4,128]{5,4,3,2,1,0:T(4,128)S(1)} %copy.103), channel_id=1, source_target_pairs={{0,32},{32,64},{64,96},{96,128},{128,160},{160,192},{192,224},{1,3... | collective-permute-start | bytes 49160 | tf_op jit(solution)/shard_map/ppermute | solution.py:24
  97.9 14.1 %collective-permute-start.15 = (f32[1,1,4,2,4,128]{5,4,3,2,1,0:T(4,128)S(1)}, f32[1,1,4,2,4,128]{5,4,3,2,1,0:T(4,128)S(1)}, u32[]{:S(2)}, u32[]{:S(2)}) collective-permute-start(f32[1,1,4,2,4,128]{5,4,3,2,1,0:T(4,128)S(1)} %copy.103), channel_id=1, source_target_pairs={{1,0},{2,1},{3,2},{4,3},{5,4},{6,5},{7,6},{8,7},{9,8},{10,9},{11,1... | collective-permute-start | bytes 49160 | tf_op jit(solution)/shard_map/ppermute | solution.py:25
  103.6 7.7 %collective-permute-start.14 = (f32[1,1,4,2,4,128]{5,4,3,2,1,0:T(4,128)S(1)}, f32[1,1,4,2,4,128]{5,4,3,2,1,0:T(4,128)S(1)}, u32[]{:S(2)}, u32[]{:S(2)}) collective-permute-start(f32[1,1,4,2,4,128]{5,4,3,2,1,0:T(4,128)S(1)} %copy.103), channel_id=1, source_target_pairs={{0,1},{1,2},{2,3},{3,4},{4,5},{5,6},{6,7},{7,8},{8,9},{9,10},{10,1... | collective-permute-start | bytes 49160 | tf_op jit(solution)/shard_map/ppermute | solution.py:24
  105.6 3.1 collective-permute-start.13
  119.1 76.6 %all-reduce.7.cloned.1.call-start = ((), (), s32[]{:S(2)}) async-start(), calls=%async_computation.2 | async-start | bytes 262144 | tf_op jit(solution)/shard_map/psum | solution.py:37
  163.9 80.8 %all-reduce.9.cloned.1.call-start = ((), (), s32[]{:S(2)}) async-start(), calls=%async_computation.3 | async-start | bytes 262144 | tf_op jit(solution)/shard_map/psum | solution.py:37
  195.7 125.3 %all-reduce.11.cloned.1.call-start = ((), (), s32[]{:S(2)}) async-start(), calls=%async_computation.4 | async-start | bytes 262144 | tf_op jit(solution)/shard_map/psum | solution.py:37
  347.3 64.7 %copy-start.11 = (s32[1024]{0:T(1024)S(1)}, s32[1024]{0:T(1024)}, u32[]{:S(2)}) copy-start(s32[1024]{0:T(1024)} %copy-done.10) | copy-start | bytes 12292
  347.3 79.9 %copy-start.9 = (s32[1024]{0:T(1024)S(1)}, s32[1024]{0:T(1024)}, u32[]{:S(2)}) copy-start(s32[1024]{0:T(1024)} %copy-done.8) | copy-start | bytes 12292
  347.3 80.6 %copy-start.7 = (f32[1,1,8,128]{3,2,1,0:T(8,128)S(1)}, f32[1,1,8,128]{3,2,1,0:T(8,128)}, u32[]{:S(2)}) copy-start(f32[1,1,8,128]{3,2,1,0:T(8,128)} %param.15) | copy-start | bytes 12292
  350.1 9.1 %collective-permute-start.16 = (f32[1,1,4,2,4,128]{5,4,3,2,1,0:T(4,128)S(1)}, f32[1,1,4,2,4,128]{5,4,3,2,1,0:T(4,128)S(1)}, u32[]{:S(2)}, u32[]{:S(2)}) collective-permute-start(f32[1,1,4,2,4,128]{5,4,3,2,1,0:T(4,128)S(1)} %copy.112), channel_id=1, source_target_pairs={{0,32},{32,64},{64,96},{96,128},{128,160},{160,192},{192,224},{1,3... | collective-permute-start | bytes 49160 | tf_op jit(solution)/shard_map/ppermute | solution.py:24
  352.0 10.7 %collective-permute-start.19 = (f32[1,1,4,2,4,128]{5,4,3,2,1,0:T(4,128)S(1)}, f32[1,1,4,2,4,128]{5,4,3,2,1,0:T(4,128)S(1)}, u32[]{:S(2)}, u32[]{:S(2)}) collective-permute-start(f32[1,1,4,2,4,128]{5,4,3,2,1,0:T(4,128)S(1)} %copy.112), channel_id=1, source_target_pairs={{1,0},{2,1},{3,2},{4,3},{5,4},{6,5},{7,6},{8,7},{9,8},{10,9},{11,1... | collective-permute-start | bytes 49160 | tf_op jit(solution)/shard_map/ppermute | solution.py:25
  354.8 7.9 %collective-permute-start.18 = (f32[1,1,4,2,4,128]{5,4,3,2,1,0:T(4,128)S(1)}, f32[1,1,4,2,4,128]{5,4,3,2,1,0:T(4,128)S(1)}, u32[]{:S(2)}, u32[]{:S(2)}) collective-permute-start(f32[1,1,4,2,4,128]{5,4,3,2,1,0:T(4,128)S(1)} %copy.112), channel_id=1, source_target_pairs={{0,1},{1,2},{2,3},{3,4},{4,5},{5,6},{6,7},{7,8},{8,9},{9,10},{10,1... | collective-permute-start | bytes 49160 | tf_op jit(solution)/shard_map/ppermute | solution.py:24
  357.8 3.1 collective-permute-start.17
  366.4 11.1 %collective-permute-start.20 = (f32[1,1,4,2,4,128]{5,4,3,2,1,0:T(4,128)S(1)}, f32[1,1,4,2,4,128]{5,4,3,2,1,0:T(4,128)S(1)}, u32[]{:S(2)}, u32[]{:S(2)}) collective-permute-start(f32[1,1,4,2,4,128]{5,4,3,2,1,0:T(4,128)S(1)} %copy.118), channel_id=1, source_target_pairs={{0,32},{32,64},{64,96},{96,128},{128,160},{160,192},{192,224},{1,3... | collective-permute-start | bytes 49160 | tf_op jit(solution)/shard_map/ppermute | solution.py:24
  368.8 13.2 %collective-permute-start.23 = (f32[1,1,4,2,4,128]{5,4,3,2,1,0:T(4,128)S(1)}, f32[1,1,4,2,4,128]{5,4,3,2,1,0:T(4,128)S(1)}, u32[]{:S(2)}, u32[]{:S(2)}) collective-permute-start(f32[1,1,4,2,4,128]{5,4,3,2,1,0:T(4,128)S(1)} %copy.118), channel_id=1, source_target_pairs={{1,0},{2,1},{3,2},{4,3},{5,4},{6,5},{7,6},{8,7},{9,8},{10,9},{11,1... | collective-permute-start | bytes 49160 | tf_op jit(solution)/shard_map/ppermute | solution.py:25
  374.3 7.7 %collective-permute-start.22 = (f32[1,1,4,2,4,128]{5,4,3,2,1,0:T(4,128)S(1)}, f32[1,1,4,2,4,128]{5,4,3,2,1,0:T(4,128)S(1)}, u32[]{:S(2)}, u32[]{:S(2)}) collective-permute-start(f32[1,1,4,2,4,128]{5,4,3,2,1,0:T(4,128)S(1)} %copy.118), channel_id=1, source_target_pairs={{0,1},{1,2},{2,3},{3,4},{4,5},{5,6},{6,7},{7,8},{8,9},{9,10},{10,1... | collective-permute-start | bytes 49160 | tf_op jit(solution)/shard_map/ppermute | solution.py:24
  376.2 3.1 collective-permute-start.21
  388.3 10.1 %collective-permute-start.24 = (f32[1,1,4,4,4,128]{5,4,3,2,1,0:T(4,128)S(1)}, f32[1,1,4,4,4,128]{5,4,3,2,1,0:T(4,128)S(1)}, u32[]{:S(2)}, u32[]{:S(2)}) collective-permute-start(f32[1,1,4,4,4,128]{5,4,3,2,1,0:T(4,128)S(1)} %bitcast.459), channel_id=1, source_target_pairs={{0,32},{32,64},{64,96},{96,128},{128,160},{160,192},{192,224},{1,3... | collective-permute-start | bytes 98312 | tf_op jit(solution)/shard_map/ppermute | solution.py:24
  389.6 13.3 %collective-permute-start.27 = (f32[1,1,4,4,4,128]{5,4,3,2,1,0:T(4,128)S(1)}, f32[1,1,4,4,4,128]{5,4,3,2,1,0:T(4,128)S(1)}, u32[]{:S(2)}, u32[]{:S(2)}) collective-permute-start(f32[1,1,4,4,4,128]{5,4,3,2,1,0:T(4,128)S(1)} %bitcast.460), channel_id=1, source_target_pairs={{1,0},{2,1},{3,2},{4,3},{5,4},{6,5},{7,6},{8,7},{9,8},{10,9},{11,1... | collective-permute-start | bytes 98312 | tf_op jit(solution)/shard_map/ppermute | solution.py:25
  395.0 7.9 %collective-permute-start.26 = (f32[1,1,4,4,4,128]{5,4,3,2,1,0:T(4,128)S(1)}, f32[1,1,4,4,4,128]{5,4,3,2,1,0:T(4,128)S(1)}, u32[]{:S(2)}, u32[]{:S(2)}) collective-permute-start(f32[1,1,4,4,4,128]{5,4,3,2,1,0:T(4,128)S(1)} %bitcast.461), channel_id=1, source_target_pairs={{0,1},{1,2},{2,3},{3,4},{4,5},{5,6},{6,7},{7,8},{8,9},{9,10},{10,1... | collective-permute-start | bytes 98312 | tf_op jit(solution)/shard_map/ppermute | solution.py:24
  396.9 3.1 collective-permute-start.25
  412.6 9.9 %collective-permute-start.28 = (f32[1,1,4,4,4,128]{5,4,3,2,1,0:T(4,128)S(1)}, f32[1,1,4,4,4,128]{5,4,3,2,1,0:T(4,128)S(1)}, u32[]{:S(2)}, u32[]{:S(2)}) collective-permute-start(f32[1,1,4,4,4,128]{5,4,3,2,1,0:T(4,128)S(1)} %bitcast.455), channel_id=1, source_target_pairs={{0,32},{32,64},{64,96},{96,128},{128,160},{160,192},{192,224},{1,3... | collective-permute-start | bytes 98312 | tf_op jit(solution)/shard_map/ppermute | solution.py:24
  413.9 13.3 %collective-permute-start.31 = (f32[1,1,4,4,4,128]{5,4,3,2,1,0:T(4,128)S(1)}, f32[1,1,4,4,4,128]{5,4,3,2,1,0:T(4,128)S(1)}, u32[]{:S(2)}, u32[]{:S(2)}) collective-permute-start(f32[1,1,4,4,4,128]{5,4,3,2,1,0:T(4,128)S(1)} %bitcast.456), channel_id=1, source_target_pairs={{1,0},{2,1},{3,2},{4,3},{5,4},{6,5},{7,6},{8,7},{9,8},{10,9},{11,1... | collective-permute-start | bytes 98312 | tf_op jit(solution)/shard_map/ppermute | solution.py:25
  419.3 7.9 %collective-permute-start.30 = (f32[1,1,4,4,4,128]{5,4,3,2,1,0:T(4,128)S(1)}, f32[1,1,4,4,4,128]{5,4,3,2,1,0:T(4,128)S(1)}, u32[]{:S(2)}, u32[]{:S(2)}) collective-permute-start(f32[1,1,4,4,4,128]{5,4,3,2,1,0:T(4,128)S(1)} %bitcast.457), channel_id=1, source_target_pairs={{0,1},{1,2},{2,3},{3,4},{4,5},{5,6},{6,7},{7,8},{8,9},{9,10},{10,1... | collective-permute-start | bytes 98312 | tf_op jit(solution)/shard_map/ppermute | solution.py:24
  421.2 3.1 collective-permute-start.29
  (1 other events, 0.6 us)
Sparse Core Ops, SparseCore 0:
  119.2 44.6 all-reduce.4
  166.5 29.1 all-reduce.6
  198.0 46.6 all-reduce.8
  246.9 74.1 all-reduce.10
